TPU v7x, 128 devices: a whole 4x4x4 slice. The times are simulated.
128 devices in a mesh: gx: 8 (over y, core), gy: 16 (over x, z).
Axes of the slice: x: 4, y: 4, z: 4, core: 2. Of those that a mesh axis runs over, the one named last changes fastest.
Arguments:
- right_side: float32 [512, 512, 512], P('gx', 'gy'), may hold values from -120 to 120
- diagonal: float32 [512, 512, 512], P('gx', 'gy'), may hold values from 0.002 to 0.2
Outputs:
- update: float32 [512, 512, 512], P('gx', 'gy')
- residual: float32 [512, 512, 512], P('gx', 'gy')
All inputs are finite; a program needn't handle non-finite values.
Results may differ from a plain program's by a relative error of at most 0.00028.
Values sent between devices are 32-bit elements; how exact they have to be, the bound alone decides.
No kernel may reach another device: no remote copies, remote signals or barrier semaphores. Data moves between devices by JAX's collectives and lax.ppermute only.
A program may use at most 128 MiB of HBM per device.

v0:
```python
import jax
import jax.numpy as jnp
from jax import lax
from jax.experimental import pallas as pl
from jax.experimental.pallas import tpu as pltpu
from jax.sharding import PartitionSpec as P


F32 = jnp.float32
BF16 = jnp.bfloat16

X, Y, Z = 64, 32, 512
DEVS_X, DEVS_Y = 8, 16
WHOLE = 512
LANES = 128
COST = 20_000_000
CHUNK = 8

XF, XM, XL, XB, XC, XROWS = 0, 384, 480, 504, 664, 680
YF, YM, YL, YB, YROWS = 0, 256, 448, 496, 528
ZROWS = 512
SCALE = (1.0, 0.25, 0.0625)


def iota(shape, axis):
    return lax.broadcasted_iota(jnp.int32, shape, axis)


def halving(depth, cols, offset=0):
    coarse = lax.shift_right_logical(iota((depth, cols), 0), 1) + offset
    return jnp.where(coarse == iota((depth, cols), 1), 0.125, 0.0).astype(BF16)


def doubling(depth, cols):
    coarse = lax.shift_right_logical(iota((depth, cols), 1), 1)
    return jnp.where(coarse == iota((depth, cols), 0), 1.0, 0.0).astype(BF16)


def times(value, table):
    high = value.astype(BF16)
    low = (value - high.astype(F32)).astype(BF16)
    return jnp.dot(high, table, preferred_element_type=F32) + jnp.dot(low, table, preferred_element_type=F32)


def in_plane(c, top, bottom):
    rows, lanes = c.shape
    row, lane = iota(c.shape, 0), iota(c.shape, 1)
    up = jnp.where(row == 0, top, pltpu.roll(c, 1, 0))
    down = jnp.where(row == rows - 1, bottom, pltpu.roll(c, rows - 1, 0))
    left = jnp.where(lane == 0, 0.0, pltpu.roll(c, 1, 1))
    right = jnp.where(lane == lanes - 1, 0.0, pltpu.roll(c, lanes - 1, 1))
    return (up + down) + (left + right)


def cols(k):
    return slice(LANES * k, LANES * (k + 1))


def take(ref, rows):
    return jnp.concatenate([ref[k, rows, :] for k in range(ref.shape[0])], axis=1)


def put(ref, rows, value):
    for k in range(ref.shape[0]):
        ref[k, rows, :] = value[:, cols(k)]


def fold(v):
    v = (v[0:8] + v[8:16]) + (v[16:24] + v[24:32])
    return (v[:, cols(0)] + v[:, cols(1)]) + (v[:, cols(2)] + v[:, cols(3)])


def send(parity, first, second, rows, low, high):
    first[rows, :] = jnp.where(parity == 0, high, low)
    second[rows, :] = jnp.where(parity == 0, low, high)


def parities():
    gx, gy = lax.axis_index("gx"), lax.axis_index("gy")
    return gx % 2, gy % 2, (gy // 2) % 2


def restrict_kernel(r_hbm, d_hbm, r_v, d_v, g_s, i_s, fx, sya, syb, sza, szb, core, rm, gm, im, s2, part,
                    cm, rl, cl, gl, il, sems):
    _, py, _ = parities()

    def copies(c):
        rows = pl.ds(c * CHUNK * Y, CHUNK * Y)
        for n, (src, dst) in enumerate(((r_hbm, r_v), (d_hbm, d_v))):
            for k in range(4):
                yield pltpu.make_async_copy(src.at[rows, pl.ds(LANES * k, LANES)], dst.at[k, rows], sems.at[n, c, k])

    for c in range(X // CHUNK):
        for one in copies(c):
            one.start()

    for k in range(4):
        g_s[k, pl.ds(0, Y), :] = jnp.zeros((Y, LANES), F32)
        g_s[k, pl.ds((X + 1) * Y, Y), :] = jnp.zeros((Y, LANES), F32)
    for k in range(2):
        gm[k, pl.ds(0, 16), :] = jnp.zeros((16, LANES), F32)
        gm[k, pl.ds(33 * 16, 16), :] = jnp.zeros((16, LANES), F32)
    half = halving(512, 256)

    def load(c, carry):
        for one in copies(c):
            one.wait()
        base = c * CHUNK * Y

        def plane(i, carry):
            rows = pl.ds(base + i * Y, Y)
            dd, rr = take(d_v, rows), take(r_v, rows)
            inv = 0.8 / (6.0 + dd)
            put(i_s, rows, inv)
            put(g_s, pl.ds(base + (i + 1) * Y, Y), inv * rr)
            return carry[0] + fold(rr), carry[1] + fold(dd)

        carry = lax.fori_loop(0, CHUNK, plane, carry)
        n = CHUNK * Y // 2
        for src, dst in ((r_v, rm), (d_v, cm)):
            pairs = jnp.concatenate(
                [src[k, pl.ds(base, n, 2), :] + src[k, pl.ds(base + 1, n, 2), :] for k in range(4)], axis=1)
            pairs = pairs.reshape(CHUNK // 2, 2, 16, Z)
            pairs = (pairs[:, 0] + pairs[:, 1]).reshape(CHUNK // 2 * 16, Z)
            put(dst, pl.ds(c * (CHUNK // 2 * 16), CHUNK // 2 * 16), times(pairs, half))
        return carry

    start = jnp.zeros((8, LANES), F32)
    part[pl.ds(0, 8), :], part[pl.ds(8, 8), :] = lax.fori_loop(0, X // CHUNK, load, (start, start))

    half = halving(256, 128)
    for src, dst in ((rm, rl), (cm, cl)):
        pairs = jnp.concatenate([src[k, pl.ds(0, 256, 2), :] + src[k, pl.ds(1, 256, 2), :] for k in range(2)], axis=1)
        pairs = pairs.reshape(16, 2, 8, 256)
        pairs = (pairs[:, 0] + pairs[:, 1]).reshape(128, 256)
        dst[...] = times(pairs, half)
    packed = 0.0
    for src, offset in ((rl, 0), (cl, 64)):
        quad = [sum(src[pl.ds(8 * f + 2 * j + e, 8, 16), :] for e in range(2) for f in range(2)) for j in range(4)]
        packed = packed + times(jnp.concatenate(quad, axis=0), halving(128, 128, offset))
    core[...] = packed
    sya[pl.ds(YB, 32), :] = packed
    syb[pl.ds(YB, 32), :] = packed

    inv = 0.8 / (0.09375 * 4.0 + cl[...])
    il[...] = inv
    gl[...] = inv * rl[...]
    for i in range(16):
        rows = pl.ds(8 * i, 8)
        c = gl[rows, :]
        total = in_plane(c, 0.0, 0.0)
        if i > 0:
            total = total + gl[pl.ds(8 * i - 8, 8), :]
        if i < 15:
            total = total + gl[pl.ds(8 * i + 8, 8), :]
        s2[rows, :] = il[rows, :] * (1.2 * rl[rows, :] + 0.0625 * total)

    def guess(i, carry):
        rows = pl.ds(64 * i, 64)
        inv = 0.8 / (1.5 + take(cm, rows))
        put(im, rows, inv)
        put(gm, pl.ds(64 * i + 16, 64), inv * take(rm, rows))
        return carry

    lax.fori_loop(0, 8, guess, 0)

    def layer(ref, rows, pad):
        return take(ref, pl.ds(rows * pad, rows))

    for hi in range(2):
        for base, g, inv, res, n, last, level in ((XF, g_s, i_s, r_v, Y, X - 1, 0), (XM, gm, im, rm, 16, 31, 1)):
            i = last * hi
            c, v = layer(g, n, i + 1), layer(inv, n, i)
            total = in_plane(c, 0.0, 0.0) + layer(g, n, i + (0 if hi else 2))
            lanes = g.shape[0]
            for a, value in enumerate((c, v, v * (1.2 * layer(res, n, i) + SCALE[level] * total))):
                for k in range(lanes):
                    fx[hi, pl.ds(base + (lanes * a + k) * n, n), :] = value[:, cols(k)]
        for a, ref in enumerate((gl, il, s2)):
            fx[hi, pl.ds(XL + a * 8, 8), :] = ref[pl.ds(hi * 15 * 8, 8), :]

    for a, (shift, pad) in enumerate(((0, 1), (0, 0), (1, 1))):
        for base, ref, n, width in ((YF, (g_s, i_s, g_s)[a], X, Y), (YM, (gm, im, gm)[a], 32, 16)):
            lanes = ref.shape[0]
            for k in range(lanes):
                late = lanes == 4 and a > 0
                start = (4 * (a - 1) + k) * n if late else base + (lanes * a + k) * n
                send(py, sza if late else sya, szb if late else syb, pl.ds(start, n),
                     ref[k, pl.ds(pad * width + shift, n, width), :],
                     ref[k, pl.ds(pad * width + width - 1 - shift, n, width), :])
        ref = (gl, il, gl)[a]
        send(py, sya, syb, pl.ds(YL + a * 16, 16), ref[pl.ds(shift, 16, 8), :], ref[pl.ds(7 - shift, 16, 8), :])


def smooth_kernel(r_v, g_s, i_s, rm, gm, im, s0, s1):
    def middle(i, carry):
        rows = pl.ds(16 * i, 16)
        c = take(gm, pl.ds(16 * i + 16, 16))
        total = in_plane(c, 0.0, 0.0) + (take(gm, rows) + take(gm, pl.ds(16 * i + 32, 16)))
        put(s1, rows, take(im, rows) * (1.2 * take(rm, rows) + 0.25 * total))
        return carry

    lax.fori_loop(0, 32, middle, 0, unroll=16)

    def fine(i, carry):
        rows = pl.ds(Y * i, Y)
        c = take(g_s, pl.ds(Y * i + Y, Y))
        total = in_plane(c, 0.0, 0.0) + (take(g_s, rows) + take(g_s, pl.ds(Y * i + 2 * Y, Y)))
        put(s0, rows, take(i_s, rows) * (1.2 * take(r_v, rows) + total))
        return carry

    lax.fori_loop(0, X, fine, 0, unroll=8)


def pick(slot, first, second, rows):
    return jnp.where(slot == 0, first[rows, :], second[rows, :])


class Halo:
    def __init__(self, **pairs):
        self.px, self.py, _ = parities()
        self.pairs = pairs

    def get(self, name, hi, start, n):
        parity = self.px if name == "rx" else self.py
        return pick(parity if hi else 1 - parity, *self.pairs[name], pl.ds(start, n))

    def layer(self, name, hi, start, n, lanes):
        return jnp.concatenate([self.get(name, hi, start + k * n, n) for k in range(lanes)], axis=1)

    def smoothed(self, along_y, hi, level, fx):
        lanes, n = 4 >> level, (X if along_y else Y) >> level
        if along_y:
            base = (YF, YM, YL)[level]
            if level == 0:
                g = self.layer("ry", hi, base, n, lanes)
                inv, beyond = [self.layer("rz", hi, a * lanes * n, n, lanes) for a in range(2)]
            else:
                g, inv, beyond = [self.layer("ry", hi, base + a * lanes * n, n, lanes) for a in range(3)]
            first, last = [self.layer("rx", xhi, XC + 7 * hi + (0, 4, 6)[level], 1, lanes) for xhi in range(2)]
            around = in_plane(g, first, last) + (beyond + self.layer("sy", hi, base, n, lanes))
            return 1.2 * g + SCALE[level] * inv * around, inv
        base = (XF, XM, XL)[level]
        inv, partly = [self.layer("rx", hi, base + a * lanes * n, n, lanes) for a in (1, 2)]
        own = jnp.concatenate([fx[hi, pl.ds(base + k * n, n), :] for k in range(lanes)], axis=1)
        return partly + SCALE[level] * inv * own, inv


def pack_kernel(fx, core, rya, ryb, r2a, r2b, block, outa, outb):
    _, _, qy = parities()
    halo = Halo(ry=(rya, ryb))
    block[pl.ds(0, 32), :] = pick(1 - qy, r2a, r2b, slice(None))
    block[pl.ds(32, 32), :] = halo.get("ry", 0, YB, 32)
    block[pl.ds(64, 32), :] = core[...]
    block[pl.ds(96, 32), :] = halo.get("ry", 1, YB, 32)
    block[pl.ds(128, 32), :] = pick(qy, r2a, r2b, slice(None))
    for out in (outa, outb):
        out[pl.ds(XB, 160), :] = block[...]
    sides = []
    for hi in range(2):
        rows, corner = [[], []], []
        for level, (base, ybase) in enumerate(((XF, YF), (XM, YM), (XL, YL))):
            lanes, n, long = 4 >> level, Y >> level, X >> level
            rows.append(fx[hi, pl.ds(base, 2 * lanes * n), :])
            edges = [[halo.get("ry", yhi, ybase + k * long + hi * (long - 1), 1) for yhi in range(2)] for k in range(lanes)]
            for k in range(lanes):
                inv = fx[hi, pl.ds(base + (lanes + k) * n, n), :]
                partly = fx[hi, pl.ds(base + (2 * lanes + k) * n, n), :]
                rows.append(partly + SCALE[level] * inv * ends(n, *edges[k]))
                for yhi in range(2):
                    rows[yhi].append(edges[k][yhi])
        corner = rows[0] + rows[1] + [jnp.zeros((2, LANES), F32)]
        sides.append((jnp.concatenate(rows[2:], axis=0), jnp.concatenate(corner, axis=0)))
    px = halo.px
    send(px, outa, outb, pl.ds(0, XB), sides[0][0], sides[1][0])
    send(px, outa, outb, pl.ds(XC, 16), sides[0][1], sides[1][1])


def ends(rows, first, last):
    row = iota((rows, LANES), 0)
    return jnp.where(row == 0, first, jnp.where(row == rows - 1, last, 0.0))


FACES = ((False, 0), (False, 1), (True, 0), (True, 1))
FACE_ROWS = (0, Y, 2 * Y, 2 * Y + X)


def coarse_kernel(s1, s2, fx, sya, syb, block, rya, ryb, rxa, rxb,
                  rep_m, fm, left_out,
                  bs, ga, gb, sz, low_s, rep_l, mid_s, fl):
    halo = Halo(sy=(sya, syb), rx=(rxa, rxb), ry=(rya, ryb))

    for n, value in enumerate((halo.get("rx", 0, XB, 160), block[...], halo.get("rx", 1, XB, 160))):
        bs[:, pl.ds(8 * n, 8), :] = value.reshape(20, 8, LANES)
    shape = (20, 24, LANES)
    live = iota(shape, 2) < 64
    both = bs[...]
    res = jnp.where(live, both, 0.0)
    coef = jnp.where(live, pltpu.roll(both, 64, 2), 0.0)
    inv = jnp.where(coef > 0.0, 0.8 / (0.09375 + coef), 0.0)
    zero = jnp.zeros((24, LANES), F32)
    for ref in (ga, gb):
        ref[0] = zero
        ref[21] = zero

    def around(ref):
        c = ref[pl.ds(1, 20)]
        total = ref[pl.ds(0, 20)] + ref[pl.ds(2, 20)]
        total = total + (pltpu.roll(c, 1, 1) + pltpu.roll(c, 23, 1))
        return c, total + (pltpu.roll(c, 1, 2) + pltpu.roll(c, LANES - 1, 2))

    ga[pl.ds(1, 20)] = inv * res
    bs[...] = inv
    now, new = ga, gb
    for _ in range(7):
        c, total = around(now)
        new[pl.ds(1, 20)] = c + bs[...] * (res - ((0.09375 + coef) * c - 0.015625 * total))
        now, new = new, now
    c, total = around(now)
    left = res - ((0.09375 + coef) * c - 0.015625 * total)
    leftover = jnp.sum(jnp.where(live[8:12, 8:16], left[8:12, 8:16], 0.0))
    sz[...] = times(now[pl.ds(8, 6)].reshape(144, LANES), doubling(LANES, LANES))

    left_out[...] = jnp.full((8, LANES), leftover, F32)

    for j in range(4):
        for e in range(2):
            for f in range(2):
                low_s[pl.ds(8 * f + 2 * j + e, 8, 16), :] = sz[pl.ds(24 * (j + 1) + 8, 8), :]
    low_s[...] = low_s[...] + s2[...]
    for hi in range(2):
        rows = pl.ds(hi * 120, 8)
        low_s[rows, :] = low_s[rows, :] + 0.0625 * fx[hi, pl.ds(XL + 8, 8), :] * halo.get("rx", hi, XL, 8)
    for hi in range(2):
        rows = pl.ds(hi * 7, 16, 8)
        low_s[rows, :] = low_s[rows, :] + 0.0625 * halo.get("sy", hi, YL + 16, 16) * halo.get("ry", hi, YL, 16)

    rep_l[pl.ds(0, 128, 2), :] = low_s[...]
    rep_l[pl.ds(1, 128, 2), :] = low_s[...]
    wide = times(rep_l[...], doubling(128, 256)).reshape(16, 1, 16, 256)
    wide = jnp.broadcast_to(wide, (16, 2, 16, 256)).reshape(512, 256)
    for k in range(2):
        mid_s[k] = wide[:, cols(k)] + s1[k]
    for hi in range(2):
        for k in range(2):
            rows = pl.ds(hi * 496, 16)
            mid_s[k, rows, :] = mid_s[k, rows, :] + (
                0.25 * fx[hi, pl.ds(XM + 32 + 16 * k, 16), :] * halo.get("rx", hi, XM + 16 * k, 16))
    for hi in range(2):
        for k in range(2):
            rows = pl.ds(hi * 15, 32, 16)
            mid_s[k, rows, :] = mid_s[k, rows, :] + (
                0.25 * halo.get("sy", hi, YM + 64 + 32 * k, 32) * halo.get("ry", hi, YM + 32 * k, 32))

    for k in range(2):
        rep_m[k, pl.ds(0, 512, 2), :] = mid_s[k]
        rep_m[k, pl.ds(1, 512, 2), :] = mid_s[k]
    for (along_y, hi), base in zip(FACES, FACE_ROWS):
        n = X if along_y else Y
        n2, n1 = n // 4, n // 2
        if along_y:
            top = sz[pl.ds(120 * hi + 8, 8), :]
        else:
            top = sz[pl.ds(24 + (16 if hi else 7), 4, 24), :]
        fl[pl.ds(0, n2 // 2, 2), :] = top
        fl[pl.ds(1, n2 // 2, 2), :] = top
        low = halo.smoothed(along_y, hi, 2, fx)[0] + fl[pl.ds(0, n2), :]
        fl[pl.ds(0, n2, 2), :] = low
        fl[pl.ds(1, n2, 2), :] = low
        wide = times(fl[pl.ds(0, n1), :], doubling(128, 256))
        middle = halo.smoothed(along_y, hi, 1, fx)[0] + wide
        for k in range(2):
            mid = middle[:, cols(k)]
            fm[k, pl.ds(base, n1, 2), :] = mid
            fm[k, pl.ds(base + 1, n1, 2), :] = mid


def fine_kernel(r_v, d_v, s0, rep_m, fm, left_in, part, fx, sya, syb, sza, szb, rya, ryb, rza, rzb, rxa, rxb,
                p, im, sums, hy):
    halo = Halo(sy=(sya, syb), sz=(sza, szb), rx=(rxa, rxb), ry=(rya, ryb), rz=(rza, rzb))
    twice = doubling(256, Z)

    def spread(i, carry):
        wide = times(take(rep_m, pl.ds(128 * i, 128)), twice).reshape(4, 1, Y, Z)
        wide = jnp.broadcast_to(wide, (4, 2, Y, Z)).reshape(8 * Y, Z)
        for k in range(4):
            p[k, pl.ds(8 * Y * i + Y, 8 * Y), :] = wide[:, cols(k)] + s0[k, pl.ds(8 * Y * i, 8 * Y), :]
        return carry

    lax.fori_loop(0, 8, spread, 0, unroll=2)
    for hi in range(2):
        for k in range(4):
            rows = pl.ds(Y + hi * (X - 1) * Y, Y)
            p[k, rows, :] = p[k, rows, :] + fx[hi, pl.ds(XF + (4 + k) * Y, Y), :] * halo.get("rx", hi, XF + k * Y, Y)
    for hi in range(2):
        for k in range(4):
            rows = pl.ds(Y + hi * (Y - 1), X, Y)
            p[k, rows, :] = p[k, rows, :] + halo.get("sz", hi, k * X, X) * halo.get("ry", hi, YF + k * X, X)

    outer = times(take(fm, pl.ds(0, 2 * (X + Y))), twice)
    for (along_y, hi), base in zip(FACES, FACE_ROWS):
        n = X if along_y else Y
        value, inv = halo.smoothed(along_y, hi, 0, fx)
        value = jnp.where(inv > 0.0, value + outer[base:base + n], 0.0)
        if along_y:
            hy[hi] = value
        else:
            put(p, pl.ds(hi * (X + 1) * Y, Y), value)

    def image(i, carry):
        rows = pl.ds(Y * i, Y)
        c = take(p, pl.ds(Y * i + Y, Y))
        around = in_plane(c, hy[0, pl.ds(i, 1), :], hy[1, pl.ds(i, 1), :])
        around = around + (take(p, rows) + take(p, pl.ds(Y * i + 2 * Y, Y)))
        dd, rr = take(d_v, rows), take(r_v, rows)
        out = (6.0 + dd) * c - around
        im[rows, :] = out
        return tuple(t + fold(v) for t, v in zip(carry, (rr * c, c * out, out)))

    start = jnp.zeros((8, LANES), F32)
    totals = lax.fori_loop(0, X, image, (start,) * 3, unroll=8)
    rz, zq, image_sum = [jnp.sum(t) for t in totals]
    totals = [rz, zq, jnp.sum(part[pl.ds(0, 8), :]), image_sum, jnp.sum(part[pl.ds(8, 8), :]), left_in[0:1, 0:1]]
    lane = iota((LANES, 8), 1)
    packed = jnp.zeros((LANES, 8), F32)
    for n, t in enumerate(totals):
        packed = jnp.where(lane == n, t, packed)
    sums[...] = packed


def final_kernel(every, r_v, d_v, p, im, update, residual):
    step = pl.program_id(0)
    gx, gy = lax.axis_index("gx"), lax.axis_index("gy")
    total = jnp.sum(every[...], axis=0, keepdims=True)
    lane8 = iota((1, 8), 1)
    rz, zq, res_sum, image_sum, coef_sum, left = [jnp.sum(jnp.where(lane8 == n, total, 0.0), axis=1, keepdims=True) for n in range(6)]
    shift = left / (coef_sum / 512.0 + 6.0 * 64.0 * 64.0 / 64.0)
    ones_sum = coef_sum + 6.0 * WHOLE * WHOLE
    alpha = (rz + shift * res_sum) / (zq + shift * (2.0 * image_sum + shift * ones_sum))
    scaled = alpha * shift
    row, lane = iota((Y, Z), 0), iota((Y, Z), 1)
    walls = jnp.where(lane == 0, 1.0, 0.0) + jnp.where(lane == Z - 1, 1.0, 0.0)
    walls = walls + jnp.where((row == 0) & (gy == 0), 1.0, 0.0)
    walls = walls + jnp.where((row == Y - 1) & (gy == DEVS_Y - 1), 1.0, 0.0)

    def plane(i, carry):
        x = step * CHUNK + i
        end = ((x == 0) & (gx == 0)) | ((x == X - 1) & (gx == DEVS_X - 1))
        rows = pl.ds(x * Y, Y)
        outside = walls + jnp.where(end, 1.0, 0.0)
        here = pl.ds(i * Y, Y)
        update[here, :] = alpha * take(p, pl.ds(x * Y + Y, Y)) + scaled
        residual[here, :] = take(r_v, rows) - alpha * im[rows, :] - scaled * (take(d_v, rows) + outside)
        return carry

    lax.fori_loop(0, CHUNK, plane, 0, unroll=2)


def f32(*shape):
    return jax.ShapeDtypeStruct(shape, F32)


def resident(*shape):
    return pltpu.VMEM(shape, F32)


def in_vmem(value):
    return pltpu.with_memory_space_constraint(value, pltpu.VMEM)


VM = pl.BlockSpec(memory_space=pltpu.VMEM)


def swap(value, axis, distance, offset):
    count = lax.axis_size(axis)
    pairs = []
    for i in range(count - distance):
        if (i // distance) % 2 == offset:
            pairs += [(i, i + distance), (i + distance, i)]
    return lax.ppermute(value, axis, pairs)


def body(right_side, diagonal):
    r = right_side.reshape(X * Y, Z)
    d = diagonal.reshape(X * Y, Z)
    vm = pltpu.VMEM
    hbm = pl.BlockSpec(memory_space=pl.ANY)
    r_v, d_v, g, inv, fx, sya, syb, sza, szb, core, rm, gm, im1, s2, part = pl.pallas_call(
        restrict_kernel,
        in_specs=[hbm, hbm],
        out_specs=[VM] * 15,
        out_shape=[resident(4, X * Y, LANES)] * 2 + [resident(4, (X + 2) * Y, LANES), resident(4, X * Y, LANES)]
        + [resident(2, XB, LANES)] + [resident(YROWS, LANES)] * 2 + [resident(ZROWS, LANES)] * 2 + [resident(32, LANES), resident(2, 512, LANES)]
        + [resident(2, 544, LANES), resident(2, 512, LANES), resident(128, 128), resident(16, LANES)],
        scratch_shapes=[vm((2, 512, LANES), F32)] + [vm((128, 128), F32)] * 4
        + [pltpu.SemaphoreType.DMA((2, X // CHUNK, 4))],
        compiler_params=pltpu.CompilerParams(vmem_limit_bytes=12 * 2**20),
        name="restrict_all",
    )(pltpu.with_memory_space_constraint(r, pltpu.HBM), pltpu.with_memory_space_constraint(d, pltpu.HBM))

    rya = swap(sya, "gy", 1, 0)
    ryb = swap(syb, "gy", 1, 1)
    r2a = swap(core, "gy", 2, 0)
    r2b = swap(core, "gy", 2, 1)
    s0, s1 = pl.pallas_call(
        smooth_kernel,
        in_specs=[VM] * 6,
        out_specs=[VM] * 2,
        out_shape=[resident(4, X * Y, LANES), resident(2, 512, LANES)],
        compiler_params=pltpu.CompilerParams(vmem_limit_bytes=4 * 2**20),
        cost_estimate=pl.CostEstimate(flops=COST, transcendentals=0, bytes_accessed=0),
        name="smooth_own",
    )(in_vmem(r_v), in_vmem(g), in_vmem(inv), in_vmem(rm), in_vmem(gm), in_vmem(im1))
    block, outa, outb = pl.pallas_call(
        pack_kernel,
        in_specs=[VM] * 6,
        out_specs=[VM] * 3,
        out_shape=[resident(160, LANES)] + [resident(XROWS, LANES)] * 2,
        compiler_params=pltpu.CompilerParams(vmem_limit_bytes=2 * 2**20),
        name="pack_faces",
    )(in_vmem(fx), in_vmem(core), rya, ryb, r2a, r2b)
    rxa = swap(outa, "gx", 1, 0)
    rxb = swap(outb, "gx", 1, 1)
    rza = swap(sza, "gy", 1, 0)
    rzb = swap(szb, "gy", 1, 1)

    rep, faces, left = pl.pallas_call(
        coarse_kernel,
        in_specs=[VM] * 10,
        out_specs=[VM] * 3,
        out_shape=[resident(2, 1024, LANES), resident(2, 2 * (X + Y), LANES), resident(8, LANES)],
        scratch_shapes=[vm((20, 24, LANES), F32), vm((22, 24, LANES), F32), vm((22, 24, LANES), F32), vm((144, LANES), F32),
                        vm((128, 128), F32), vm((256, 128), F32), vm((2, 512, LANES), F32), vm((32, LANES), F32)],
        compiler_params=pltpu.CompilerParams(vmem_limit_bytes=8 * 2**20),
        cost_estimate=pl.CostEstimate(flops=COST, transcendentals=0, bytes_accessed=0),
        name="solve_coarse",
    )(in_vmem(s1), in_vmem(s2), in_vmem(fx), in_vmem(sya), in_vmem(syb), in_vmem(block), rya, ryb, rxa, rxb)
    p, im, sums = pl.pallas_call(
        fine_kernel,
        in_specs=[VM] * 18,
        out_specs=[VM] * 3,
        out_shape=[resident(4, (X + 2) * Y, LANES), resident(X * Y, Z), f32(LANES, 8)],
        scratch_shapes=[vm((2, X, Z), F32)],
        compiler_params=pltpu.CompilerParams(vmem_limit_bytes=8 * 2**20),
        name="solve_fine",
    )(in_vmem(r_v), in_vmem(d_v), in_vmem(s0), in_vmem(rep), in_vmem(faces), in_vmem(left),
      in_vmem(part), in_vmem(fx), in_vmem(sya), in_vmem(syb), in_vmem(sza), in_vmem(szb), rya, ryb, rza, rzb, rxa, rxb)

    every = lax.all_to_all(sums, ("gx", "gy"), 0, 0, tiled=True)
    blocks = pl.BlockSpec((CHUNK * Y, Z), lambda i: (i, 0))
    update, residual = pl.pallas_call(
        final_kernel,
        grid=(X // CHUNK,),
        in_specs=[VM] * 5,
        out_specs=[blocks, blocks],
        out_shape=[f32(X * Y, Z), f32(X * Y, Z)],
        compiler_params=pltpu.CompilerParams(vmem_limit_bytes=8 * 2**20),
        name="scale_outputs",
    )(every, in_vmem(r_v), in_vmem(d_v), in_vmem(p), in_vmem(im))
    return update.reshape(X, Y, Z), residual.reshape(X, Y, Z)


def solution(mesh):
    return jax.shard_map(
        body,
        mesh=mesh,
        in_specs=(P("gx", "gy", None), P("gx", "gy", None)),
        out_specs=(P("gx", "gy", None), P("gx", "gy", None)),
        check_vma=False,
    )
```

profile of v0, /device:TPU:1, one launch (start us, length us, event | category | flops | bytes accessed | tf_op | source)
XLA Modules:
  0.0 69.4 jit_solution(16434204292374857977)
XLA Ops:
  0.6 6.4 %restrict_all.1 = (f32[4,2048,128]{2,1,0:T(8,128)S(1)}, f32[4,2048,128]{2,1,0:T(8,128)S(1)}, f32[4,2112,128]{2,1,0:T(8,128)S(1)}, f32[4,2048,128]{2,1,0:T(8,128)...) custom-call(f32[2048,512]{1,0:T(8,128)} %bitcast.10, ...), custom_call_target="tpu_custom_call" | custom-call | tf_op jit(solution)/shard_map/restrict_all/pallas_call | solution.py:488
  7.1 2.5 %collective-permute-start = (f32[528,128]{1,0:T(8,128)S(1)}, f32[528,128]{1,0:T(8,128)S(1)}, u32[]{:S(2)}, u32[]{:S(2)}) collective-permute-start(f32[528,128]{1,0:T(8,128)S(1)} %get-tuple-element.41.sya), channel_id=1, source_target_pairs={{0,1},{1,0},{2,3},{3,2},{4,5},{5,4},{6,7},{7,6},{8,9},{9,8},{10,11... | collective-permute-start | bytes 811016 | tf_op jit(solution)/shard_map/ppermute | solution.py:480
  9.6 0.7 collective-permute-start.1
  10.3 0.7 collective-permute-start.3
  10.9 8.7 %collective-permute-start.2 = (f32[32,128]{1,0:T(8,128)S(1)}, f32[32,128]{1,0:T(8,128)S(1)}, u32[]{:S(2)}, u32[]{:S(2)}) collective-permute-start(f32[32,128]{1,0:T(8,128)S(1)} %get-tuple-element.43.core), channel_id=1, source_target_pairs={{0,2},{2,0},{1,3},{3,1},{4,6},{6,4},{5,7},{7,5},{8,10},{10,8},{9,1... | collective-permute-start | bytes 49160 | tf_op jit(solution)/shard_map/ppermute | solution.py:480
  19.6 0.0 collective-permute-done.3.r2b
  19.6 1.1 %collective-permute-done.2.r2a = f32[32,128]{1,0:T(8,128)S(1)} collective-permute-done((f32[32,128]{1,0:T(8,128)S(1)}, f32[32,128]{1,0:T(8,128)S(1)}, u32[]{:S(2)}, u32[]{:S(2)}) %collective-permute-start.2) | collective-permute-done | bytes 16416 | tf_op jit(solution)/shard_map/ppermute | solution.py:480
  20.7 0.0 collective-permute-done.rya
  20.7 0.0 collective-permute-done.1.ryb
  20.7 0.1 pack_faces.1
  20.9 2.5 %collective-permute-start.4 = (f32[680,128]{1,0:T(8,128)S(1)}, f32[680,128]{1,0:T(8,128)S(1)}, u32[]{:S(2)}, u32[]{:S(2)}) collective-permute-start(f32[680,128]{1,0:T(8,128)S(1)} %get-tuple-element.45), channel_id=1, source_target_pairs={{0,16},{16,0},{32,48},{48,32},{64,80},{80,64},{96,112},{112,96},{1... | collective-permute-start | bytes 1044488 | tf_op jit(solution)/shard_map/ppermute | solution.py:480
  23.3 3.1 %collective-permute-start.5 = (f32[680,128]{1,0:T(8,128)S(1)}, f32[680,128]{1,0:T(8,128)S(1)}, u32[]{:S(2)}, u32[]{:S(2)}) collective-permute-start(f32[680,128]{1,0:T(8,128)S(1)} %get-tuple-element.46), channel_id=1, source_target_pairs={{16,32},{32,16},{48,64},{64,48},{80,96},{96,80},{17,33},{33,17},{4... | collective-permute-start | bytes 1044488 | tf_op jit(solution)/shard_map/ppermute | solution.py:480
  26.4 0.8 %collective-permute-start.6 = (f32[512,128]{1,0:T(8,128)S(1)}, f32[512,128]{1,0:T(8,128)S(1)}, u32[]{:S(2)}, u32[]{:S(2)}) collective-permute-start(f32[512,128]{1,0:T(8,128)S(1)} %get-tuple-element.51.sza), channel_id=1, source_target_pairs={{0,1},{1,0},{2,3},{3,2},{4,5},{5,4},{6,7},{7,6},{8,9},{9,8},{10,11... | collective-permute-start | bytes 786440 | tf_op jit(solution)/shard_map/ppermute | solution.py:480
  27.3 0.7 collective-permute-start.7
  27.9 3.6 %smooth_own.1 = (f32[4,2048,128]{2,1,0:T(8,128)S(1)}, f32[2,512,128]{2,1,0:T(8,128)S(1)}) custom-call(f32[4,2048,128]{2,1,0:T(8,128)S(1)} %get-tuple-element.30.r_v, f32[4,2112,128]{2,1,0:T(8,128)S(1)} %get-tuple-element.32.g_s, f32[4,2048,128]{2,1,0:T(8,128)S(1)} %get-tuple-element.33.i_s, f32[2,512,128]{2,1,0:T(8,128)S(1)} %get-tuple-element.34.rm, ...), custom_call_target="tpu_custom_call" | custom-call | flops 20000000 | tf_op jit(solution)/shard_map/smooth_own/pallas_call | solution.py:505
  31.6 0.0 collective-permute-done.4.rxa
  31.6 0.3 collective-permute-done.5.rxb
  31.9 1.4 %solve_coarse.1 = (f32[2,1024,128]{2,1,0:T(8,128)S(1)}, f32[2,192,128]{2,1,0:T(8,128)S(1)}, f32[8,128]{1,0:T(8,128)S(1)}) custom-call(f32[2,512,128]{2,1,0:T(8,128)S(1)} %get-tuple-element.38.s1, f32[128,128]{1,0:T(8,128)S(1)} %get-tuple-element.39.s2, f32[2,504,128]{2,1,0:T(8,128)S(1)} %get-tuple-element.40.fx, f32[528,128]{1,0:T(8,128)S(1)} %get-tuple-element.41.sya, ...), custom_call_target="tpu_custom_call" | custom-call | flops 20000000 | tf_op jit(solution)/shard_map/solve_coarse/pallas_call | solution.py:527
  33.3 0.0 collective-permute-done.6.rza
  33.3 0.0 collective-permute-done.7.rzb
  33.3 5.9 %solve_fine.1 = (f32[4,2112,128]{2,1,0:T(8,128)S(1)}, f32[2048,512]{1,0:T(8,128)S(1)}, f32[128,8]{1,0:T(8,128)S(1)}) custom-call(f32[4,2048,128]{2,1,0:T(8,128)S(1)} %get-tuple-element.30.r_v, f32[4,2048,128]{2,1,0:T(8,128)S(1)} %get-tuple-element.31.d_v, f32[4,2048,128]{2,1,0:T(8,128)S(1)} %get-tuple-element.37.s0, ...), custom_call_target="tpu_custom_call" | custom-call | tf_op jit(solution)/shard_map/solve_fine/pallas_call | solution.py:538
  39.2 24.7 %all_to_all.11 = f32[128,1,8]{2,1,0:T(1,128)S(1)} all-to-all(f32[128,1,8]{2,1,0:T(1,128)S(1)} %bitcast.9), channel_id=1, replica_groups=mesh['gx'=8,'gy'=16] {'gx','gy'}, dimensions={0} | all-to-all | bytes 8192 | tf_op jit(solution)/shard_map/all_to_all | solution.py:549
  64.0 5.4 %scale_outputs.1 = (f32[2048,512]{1,0:T(8,128)}, f32[2048,512]{1,0:T(8,128)}) custom-call(f32[128,8]{1,0:T(8,128)S(1)} %bitcast.8, f32[4,2048,128]{2,1,0:T(8,128)S(1)} %get-tuple-element.30.r_v, f32[4,2048,128]{2,1,0:T(8,128)S(1)} %get-tuple-element.31.d_v, f32[4,2112,128]{2,1,0:T(8,128)S(1)} %get-tuple-element.54.p, f32[2048,512]{1,0:T(8,128)S(1)} %get-tuple-element.55.im), custom_call_target="tpu_custom_call" | custom-call | tf_op jit(solution)/shard_map/scale_outputs/pallas_call | solution.py:551
Async XLA Ops:
  7.1 13.7 %collective-permute-start = (f32[528,128]{1,0:T(8,128)S(1)}, f32[528,128]{1,0:T(8,128)S(1)}, u32[]{:S(2)}, u32[]{:S(2)}) collective-permute-start(f32[528,128]{1,0:T(8,128)S(1)} %get-tuple-element.41.sya), channel_id=1, source_target_pairs={{0,1},{1,0},{2,3},{3,2},{4,5},{5,4},{6,7},{7,6},{8,9},{9,8},{10,11... | collective-permute-start | bytes 811016 | tf_op jit(solution)/shard_map/ppermute | solution.py:480
  9.6 11.1 %collective-permute-start.1 = (f32[528,128]{1,0:T(8,128)S(1)}, f32[528,128]{1,0:T(8,128)S(1)}, u32[]{:S(2)}, u32[]{:S(2)}) collective-permute-start(f32[528,128]{1,0:T(8,128)S(1)} %get-tuple-element.42.syb), channel_id=1, source_target_pairs={{1,2},{2,1},{3,4},{4,3},{5,6},{6,5},{7,8},{8,7},{9,10},{10,9},{11,... | collective-permute-start | bytes 811016 | tf_op jit(solution)/shard_map/ppermute | solution.py:480
  10.3 9.3 %collective-permute-start.3 = (f32[32,128]{1,0:T(8,128)S(1)}, f32[32,128]{1,0:T(8,128)S(1)}, u32[]{:S(2)}, u32[]{:S(2)}) collective-permute-start(f32[32,128]{1,0:T(8,128)S(1)} %get-tuple-element.43.core), channel_id=1, source_target_pairs={{2,4},{4,2},{3,5},{5,3},{6,8},{8,6},{7,9},{9,7},{10,12},{12,10},{1... | collective-permute-start | bytes 49160 | tf_op jit(solution)/shard_map/ppermute | solution.py:480
  10.9 9.8 %collective-permute-start.2 = (f32[32,128]{1,0:T(8,128)S(1)}, f32[32,128]{1,0:T(8,128)S(1)}, u32[]{:S(2)}, u32[]{:S(2)}) collective-permute-start(f32[32,128]{1,0:T(8,128)S(1)} %get-tuple-element.43.core), channel_id=1, source_target_pairs={{0,2},{2,0},{1,3},{3,1},{4,6},{6,4},{5,7},{7,5},{8,10},{10,8},{9,1... | collective-permute-start | bytes 49160 | tf_op jit(solution)/shard_map/ppermute | solution.py:480
  20.9 10.8 %collective-permute-start.4 = (f32[680,128]{1,0:T(8,128)S(1)}, f32[680,128]{1,0:T(8,128)S(1)}, u32[]{:S(2)}, u32[]{:S(2)}) collective-permute-start(f32[680,128]{1,0:T(8,128)S(1)} %get-tuple-element.45), channel_id=1, source_target_pairs={{0,16},{16,0},{32,48},{48,32},{64,80},{80,64},{96,112},{112,96},{1... | collective-permute-start | bytes 1044488 | tf_op jit(solution)/shard_map/ppermute | solution.py:480
  23.3 8.6 %collective-permute-start.5 = (f32[680,128]{1,0:T(8,128)S(1)}, f32[680,128]{1,0:T(8,128)S(1)}, u32[]{:S(2)}, u32[]{:S(2)}) collective-permute-start(f32[680,128]{1,0:T(8,128)S(1)} %get-tuple-element.46), channel_id=1, source_target_pairs={{16,32},{32,16},{48,64},{64,48},{80,96},{96,80},{17,33},{33,17},{4... | collective-permute-start | bytes 1044488 | tf_op jit(solution)/shard_map/ppermute | solution.py:480
  26.4 6.9 %collective-permute-start.6 = (f32[512,128]{1,0:T(8,128)S(1)}, f32[512,128]{1,0:T(8,128)S(1)}, u32[]{:S(2)}, u32[]{:S(2)}) collective-permute-start(f32[512,128]{1,0:T(8,128)S(1)} %get-tuple-element.51.sza), channel_id=1, source_target_pairs={{0,1},{1,0},{2,3},{3,2},{4,5},{5,4},{6,7},{7,6},{8,9},{9,8},{10,11... | collective-permute-start | bytes 786440 | tf_op jit(solution)/shard_map/ppermute | solution.py:480
  27.3 6.0 %collective-permute-start.7 = (f32[512,128]{1,0:T(8,128)S(1)}, f32[512,128]{1,0:T(8,128)S(1)}, u32[]{:S(2)}, u32[]{:S(2)}) collective-permute-start(f32[512,128]{1,0:T(8,128)S(1)} %get-tuple-element.52.szb), channel_id=1, source_target_pairs={{1,2},{2,1},{3,4},{4,3},{5,6},{6,5},{7,8},{8,7},{9,10},{10,9},{11,... | collective-permute-start | bytes 786440 | tf_op jit(solution)/shard_map/ppermute | solution.py:480
where the time goes:
time: 69.6 us; the launch traced here: 69.4 us
  blocking collectives  24.7 us (35%)
  Pallas kernels  22.9 us (33%)
  starting transfers between devices  19.6 us (28%)
  waiting for transfers between devices  1.45 us (2%)
  between operations  0.73 us (1%)
    all_to_all x1, blocking collectives, body(): every = lax.all_to_all(sums, ('gx', 'gy'), 0, 0, tiled=True)  24.7 us
    ppermute x8, starting transfers between devices, swap(): return lax.ppermute(value, axis, pairs)  19.6 us
    pallas_call x1, Pallas kernels, body(): pl.pallas_call(restrict_kernel, in_specs=[hbm, hbm], out_specs=[VM] * 15,...  6.42 us
    pallas_call x1, Pallas kernels, body(): pl.pallas_call(fine_kernel, in_specs=[VM] * 18, out_specs=[VM] * 3, out_s...  5.92 us
    pallas_call x1, Pallas kernels, body(): pl.pallas_call(final_kernel, grid=(X // CHUNK,), in_specs=[VM] * 5, out_s...  5.43 us
    pallas_call x1, Pallas kernels, body(): pl.pallas_call(smooth_kernel, in_specs=[VM] * 6, out_specs=[VM] * 2, out_...  3.64 us
    ppermute x8, waiting for transfers between devices, swap(): return lax.ppermute(value, axis, pairs)  1.45 us
  transfers between devices with their start and end apart: 8, of which 2 were waited for; matrix products, arithmetic and copies ran while one was open for 0% of the time, Pallas kernels for 7%

commit v1 on v0

--- a/solution.py
+++ b/solution.py
@@ -14,7 +14,8 @@
 WHOLE = 512
 LANES = 128
 COST = 20_000_000
-CHUNK = 8
+CHUNK = 16
+OUT = 16
 
 XF, XM, XL, XB, XC, XROWS = 0, 384, 480, 504, 664, 680
 YF, YM, YL, YB, YROWS = 0, 256, 448, 496, 528
@@ -70,20 +71,19 @@
     return (v[:, cols(0)] + v[:, cols(1)]) + (v[:, cols(2)] + v[:, cols(3)])
 
 
-def send(parity, first, second, rows, low, high):
-    first[rows, :] = jnp.where(parity == 0, high, low)
-    second[rows, :] = jnp.where(parity == 0, low, high)
-
-
-def parities():
-    gx, gy = lax.axis_index("gx"), lax.axis_index("gy")
-    return gx % 2, gy % 2, (gy // 2) % 2
+def send(up, down, rows, low, high):
+    up[rows, :] = high
+    down[rows, :] = low
+
+
+def beside(value, hi, axis, distance=1):
+    index = lax.axis_index(axis)
+    outside = index + distance >= lax.axis_size(axis) if hi else index < distance
+    return jnp.where(outside, 0.0, value)
 
 
 def restrict_kernel(r_hbm, d_hbm, r_v, d_v, g_s, i_s, fx, sya, syb, sza, szb, core, rm, gm, im, s2, part,
                     cm, rl, cl, gl, il, sems):
-    _, py, _ = parities()
-
     def copies(c):
         rows = pl.ds(c * CHUNK * Y, CHUNK * Y)
         for n, (src, dst) in enumerate(((r_hbm, r_v), (d_hbm, d_v))):
@@ -115,7 +115,7 @@
             put(g_s, pl.ds(base + (i + 1) * Y, Y), inv * rr)
             return carry[0] + fold(rr), carry[1] + fold(dd)
 
-        carry = lax.fori_loop(0, CHUNK, plane, carry)
+        carry = lax.fori_loop(0, CHUNK, plane, carry, unroll=4)
         n = CHUNK * Y // 2
         for src, dst in ((r_v, rm), (d_v, cm)):
             pairs = jnp.concatenate(
@@ -185,11 +185,11 @@
             for k in range(lanes):
                 late = lanes == 4 and a > 0
                 start = (4 * (a - 1) + k) * n if late else base + (lanes * a + k) * n
-                send(py, sza if late else sya, szb if late else syb, pl.ds(start, n),
+                send(sza if late else sya, szb if late else syb, pl.ds(start, n),
                      ref[k, pl.ds(pad * width + shift, n, width), :],
                      ref[k, pl.ds(pad * width + width - 1 - shift, n, width), :])
         ref = (gl, il, gl)[a]
-        send(py, sya, syb, pl.ds(YL + a * 16, 16), ref[pl.ds(shift, 16, 8), :], ref[pl.ds(7 - shift, 16, 8), :])
+        send(sya, syb, pl.ds(YL + a * 16, 16), ref[pl.ds(shift, 16, 8), :], ref[pl.ds(7 - shift, 16, 8), :])
 
 
 def smooth_kernel(r_v, g_s, i_s, rm, gm, im, s0, s1):
@@ -212,18 +212,15 @@
     lax.fori_loop(0, X, fine, 0, unroll=8)
 
 
-def pick(slot, first, second, rows):
-    return jnp.where(slot == 0, first[rows, :], second[rows, :])
-
-
 class Halo:
     def __init__(self, **pairs):
-        self.px, self.py, _ = parities()
         self.pairs = pairs
 
     def get(self, name, hi, start, n):
-        parity = self.px if name == "rx" else self.py
-        return pick(parity if hi else 1 - parity, *self.pairs[name], pl.ds(start, n))
+        value = self.pairs[name][1 - hi][pl.ds(start, n), :]
+        if name[0] == "s":
+            return value
+        return beside(value, hi, "gx" if name == "rx" else "gy")
 
     def layer(self, name, hi, start, n, lanes):
         return jnp.concatenate([self.get(name, hi, start + k * n, n) for k in range(lanes)], axis=1)
@@ -247,13 +244,12 @@
 
 
 def pack_kernel(fx, core, rya, ryb, r2a, r2b, block, outa, outb):
-    _, _, qy = parities()
     halo = Halo(ry=(rya, ryb))
-    block[pl.ds(0, 32), :] = pick(1 - qy, r2a, r2b, slice(None))
+    block[pl.ds(0, 32), :] = beside(r2b[...], 0, "gy", 2)
     block[pl.ds(32, 32), :] = halo.get("ry", 0, YB, 32)
     block[pl.ds(64, 32), :] = core[...]
     block[pl.ds(96, 32), :] = halo.get("ry", 1, YB, 32)
-    block[pl.ds(128, 32), :] = pick(qy, r2a, r2b, slice(None))
+    block[pl.ds(128, 32), :] = beside(r2a[...], 1, "gy", 2)
     for out in (outa, outb):
         out[pl.ds(XB, 160), :] = block[...]
     sides = []
@@ -271,9 +267,8 @@
                     rows[yhi].append(edges[k][yhi])
         corner = rows[0] + rows[1] + [jnp.zeros((2, LANES), F32)]
         sides.append((jnp.concatenate(rows[2:], axis=0), jnp.concatenate(corner, axis=0)))
-    px = halo.px
-    send(px, outa, outb, pl.ds(0, XB), sides[0][0], sides[1][0])
-    send(px, outa, outb, pl.ds(XC, 16), sides[0][1], sides[1][1])
+    send(outa, outb, pl.ds(0, XB), sides[0][0], sides[1][0])
+    send(outa, outb, pl.ds(XC, 16), sides[0][1], sides[1][1])
 
 
 def ends(rows, first, last):
@@ -444,7 +439,7 @@
     walls = walls + jnp.where((row == Y - 1) & (gy == DEVS_Y - 1), 1.0, 0.0)
 
     def plane(i, carry):
-        x = step * CHUNK + i
+        x = step * OUT + i
         end = ((x == 0) & (gx == 0)) | ((x == X - 1) & (gx == DEVS_X - 1))
         rows = pl.ds(x * Y, Y)
         outside = walls + jnp.where(end, 1.0, 0.0)
@@ -453,7 +448,7 @@
         residual[here, :] = take(r_v, rows) - alpha * im[rows, :] - scaled * (take(d_v, rows) + outside)
         return carry
 
-    lax.fori_loop(0, CHUNK, plane, 0, unroll=2)
+    lax.fori_loop(0, OUT, plane, 0, unroll=8)
 
 
 def f32(*shape):
@@ -471,13 +466,9 @@
 VM = pl.BlockSpec(memory_space=pltpu.VMEM)
 
 
-def swap(value, axis, distance, offset):
+def shift(value, axis, distance):
     count = lax.axis_size(axis)
-    pairs = []
-    for i in range(count - distance):
-        if (i // distance) % 2 == offset:
-            pairs += [(i, i + distance), (i + distance, i)]
-    return lax.ppermute(value, axis, pairs)
+    return lax.ppermute(value, axis, [(i, (i + distance) % count) for i in range(count)])
 
 
 def body(right_side, diagonal):
@@ -498,10 +489,10 @@
         name="restrict_all",
     )(pltpu.with_memory_space_constraint(r, pltpu.HBM), pltpu.with_memory_space_constraint(d, pltpu.HBM))
 
-    rya = swap(sya, "gy", 1, 0)
-    ryb = swap(syb, "gy", 1, 1)
-    r2a = swap(core, "gy", 2, 0)
-    r2b = swap(core, "gy", 2, 1)
+    rya = shift(syb, "gy", -1)
+    ryb = shift(sya, "gy", 1)
+    r2a = shift(core, "gy", -2)
+    r2b = shift(core, "gy", 2)
     s0, s1 = pl.pallas_call(
         smooth_kernel,
         in_specs=[VM] * 6,
@@ -519,10 +510,10 @@
         compiler_params=pltpu.CompilerParams(vmem_limit_bytes=2 * 2**20),
         name="pack_faces",
     )(in_vmem(fx), in_vmem(core), rya, ryb, r2a, r2b)
-    rxa = swap(outa, "gx", 1, 0)
-    rxb = swap(outb, "gx", 1, 1)
-    rza = swap(sza, "gy", 1, 0)
-    rzb = swap(szb, "gy", 1, 1)
+    rxa = shift(outb, "gx", -1)
+    rxb = shift(outa, "gx", 1)
+    rza = shift(szb, "gy", -1)
+    rzb = shift(sza, "gy", 1)
 
     rep, faces, left = pl.pallas_call(
         coarse_kernel,
@@ -547,14 +538,14 @@
       in_vmem(part), in_vmem(fx), in_vmem(sya), in_vmem(syb), in_vmem(sza), in_vmem(szb), rya, ryb, rza, rzb, rxa, rxb)
 
     every = lax.all_to_all(sums, ("gx", "gy"), 0, 0, tiled=True)
-    blocks = pl.BlockSpec((CHUNK * Y, Z), lambda i: (i, 0))
+    blocks = pl.BlockSpec((OUT * Y, Z), lambda i: (i, 0))
     update, residual = pl.pallas_call(
         final_kernel,
-        grid=(X // CHUNK,),
+        grid=(X // OUT,),
         in_specs=[VM] * 5,
         out_specs=[blocks, blocks],
         out_shape=[f32(X * Y, Z), f32(X * Y, Z)],
-        compiler_params=pltpu.CompilerParams(vmem_limit_bytes=8 * 2**20),
+        compiler_params=pltpu.CompilerParams(vmem_limit_bytes=10 * 2**20),
         name="scale_outputs",
     )(every, in_vmem(r_v), in_vmem(d_v), in_vmem(p), in_vmem(im))
     return update.reshape(X, Y, Z), residual.reshape(X, Y, Z)

time: 69.6 us -> 62.6 us (0.90)
  blocking collectives: 24.7 us -> 18.7 us
  Pallas kernels: 22.9 us -> 20.6 us
  waiting for transfers between devices: 1.45 us -> 2.67 us
    all_to_all x1, blocking collectives: 24.7 us -> 18.7 us  [body(): every = lax.all_to_all(sums, ('gx', 'gy'), 0, 0, tiled=True)]
    ppermute x8, waiting for transfers between devices: 1.45 us -> 2.67 us  [shift(): lax.ppermute(value, axis, [(i, (i + distance) % count) for i in range(cou...]
    pallas_call x1, Pallas kernels: 5.43 us -> 4.3 us  [body(): pl.pallas_call(final_kernel, grid=(X // OUT,), in_specs=[VM] * 5, out_spe...]
    pallas_call x1, Pallas kernels: 6.42 us -> 5.55 us  [body(): pl.pallas_call(restrict_kernel, in_specs=[hbm, hbm], out_specs=[VM] * 15,...]
  transfers between devices with their start and end apart: 8 -> 8, of which waited for: 2 -> 2; matrix products, arithmetic and copies ran while one was open for 0% -> 0% of each run, Pallas kernels for 7% -> 8%
where the time goes in v1:
time: 62.6 us; the launch traced here: 62.5 us
  Pallas kernels  20.6 us (33%)
  starting transfers between devices  19.8 us (32%)
  blocking collectives  18.7 us (30%)
  waiting for transfers between devices  2.67 us (4%)
  between operations  0.69 us (1%)
    ppermute x8, starting transfers between devices, shift(): lax.ppermute(value, axis, [(i, (i + distance) % count) for i in range(cou...  19.8 us
    all_to_all x1, blocking collectives, body(): every = lax.all_to_all(sums, ('gx', 'gy'), 0, 0, tiled=True)  18.7 us
    pallas_call x1, Pallas kernels, body(): pl.pallas_call(fine_kernel, in_specs=[VM] * 18, out_specs=[VM] * 3, out_s...  5.68 us
    pallas_call x1, Pallas kernels, body(): pl.pallas_call(restrict_kernel, in_specs=[hbm, hbm], out_specs=[VM] * 15,...  5.55 us
    pallas_call x1, Pallas kernels, body(): pl.pallas_call(final_kernel, grid=(X // OUT,), in_specs=[VM] * 5, out_spe...  4.3 us
    pallas_call x1, Pallas kernels, body(): pl.pallas_call(smooth_kernel, in_specs=[VM] * 6, out_specs=[VM] * 2, out_...  3.64 us
    ppermute x8, waiting for transfers between devices, shift(): lax.ppermute(value, axis, [(i, (i + distance) % count) for i in range(cou...  2.67 us
    pallas_call x1, Pallas kernels, body(): pl.pallas_call(coarse_kernel, in_specs=[VM] * 10, out_specs=[VM] * 3, out...  1.37 us
  transfers between devices with their start and end apart: 8, of which 2 were waited for; matrix products, arithmetic and copies ran while one was open for 0% of the time, Pallas kernels for 8%

profile of v1, /device:TPU:1, one launch (start us, length us, event | category | flops | bytes accessed | tf_op | source)
XLA Modules:
  0.0 62.5 jit_solution(8028755562673367921)
XLA Ops:
  0.6 5.5 %restrict_all.1 = (f32[4,2048,128]{2,1,0:T(8,128)S(1)}, f32[4,2048,128]{2,1,0:T(8,128)S(1)}, f32[4,2112,128]{2,1,0:T(8,128)S(1)}, f32[4,2048,128]{2,1,0:T(8,128)...) custom-call(f32[2048,512]{1,0:T(8,128)} %bitcast.10, ...), custom_call_target="tpu_custom_call" | custom-call | tf_op jit(solution)/shard_map/restrict_all/pallas_call | solution.py:479
  6.2 2.5 %collective-permute-start.1 = (f32[528,128]{1,0:T(8,128)S(1)}, f32[528,128]{1,0:T(8,128)S(1)}, u32[]{:S(2)}, u32[]{:S(2)}) collective-permute-start(f32[528,128]{1,0:T(8,128)S(1)} %get-tuple-element.41.sya), channel_id=1, source_target_pairs={{0,1},{1,2},{2,3},{3,4},{4,5},{5,6},{6,7},{7,8},{8,9},{9,10},{10,1... | collective-permute-start | bytes 811016 | tf_op jit(solution)/shard_map/ppermute | solution.py:471
  8.7 4.4 %collective-permute-start = (f32[528,128]{1,0:T(8,128)S(1)}, f32[528,128]{1,0:T(8,128)S(1)}, u32[]{:S(2)}, u32[]{:S(2)}) collective-permute-start(f32[528,128]{1,0:T(8,128)S(1)} %get-tuple-element.42.syb), channel_id=1, source_target_pairs={{0,15},{1,0},{2,1},{3,2},{4,3},{5,4},{6,5},{7,6},{8,7},{9,8},{10,9... | collective-permute-start | bytes 811016 | tf_op jit(solution)/shard_map/ppermute | solution.py:471
  13.1 0.0 collective-permute-start.3
  13.1 5.1 %collective-permute-start.2 = (f32[32,128]{1,0:T(8,128)S(1)}, f32[32,128]{1,0:T(8,128)S(1)}, u32[]{:S(2)}, u32[]{:S(2)}) collective-permute-start(f32[32,128]{1,0:T(8,128)S(1)} %get-tuple-element.43.core), channel_id=1, source_target_pairs={{0,14},{1,15},{2,0},{3,1},{4,2},{5,3},{6,4},{7,5},{8,6},{9,7},{10,... | collective-permute-start | bytes 49160 | tf_op jit(solution)/shard_map/ppermute | solution.py:471
  18.2 1.5 %collective-permute-done.3.r2b = f32[32,128]{1,0:T(8,128)S(1)} collective-permute-done((f32[32,128]{1,0:T(8,128)S(1)}, f32[32,128]{1,0:T(8,128)S(1)}, u32[]{:S(2)}, u32[]{:S(2)}) %collective-permute-start.3) | collective-permute-done | bytes 16416 | tf_op jit(solution)/shard_map/ppermute | solution.py:471
  19.7 0.0 collective-permute-done.2.r2a
  19.7 0.0 collective-permute-done.1.ryb
  19.7 0.0 collective-permute-done.rya
  19.7 0.1 pack_faces.1
  19.7 1.8 %collective-permute-start.4 = (f32[680,128]{1,0:T(8,128)S(1)}, f32[680,128]{1,0:T(8,128)S(1)}, u32[]{:S(2)}, u32[]{:S(2)}) collective-permute-start(f32[680,128]{1,0:T(8,128)S(1)} %get-tuple-element.45), channel_id=1, source_target_pairs={{0,112},{16,0},{32,16},{48,32},{64,48},{80,64},{96,80},{112,96},{1... | collective-permute-start | bytes 1044488 | tf_op jit(solution)/shard_map/ppermute | solution.py:471
  21.5 1.2 %collective-permute-start.5 = (f32[680,128]{1,0:T(8,128)S(1)}, f32[680,128]{1,0:T(8,128)S(1)}, u32[]{:S(2)}, u32[]{:S(2)}) collective-permute-start(f32[680,128]{1,0:T(8,128)S(1)} %get-tuple-element.46), channel_id=1, source_target_pairs={{0,16},{16,32},{32,48},{48,64},{64,80},{80,96},{96,112},{112,0},{1... | collective-permute-start | bytes 1044488 | tf_op jit(solution)/shard_map/ppermute | solution.py:471
  22.7 0.0 collective-permute-start.7
  22.7 4.8 %collective-permute-start.6 = (f32[512,128]{1,0:T(8,128)S(1)}, f32[512,128]{1,0:T(8,128)S(1)}, u32[]{:S(2)}, u32[]{:S(2)}) collective-permute-start(f32[512,128]{1,0:T(8,128)S(1)} %get-tuple-element.52.szb), channel_id=1, source_target_pairs={{0,15},{1,0},{2,1},{3,2},{4,3},{5,4},{6,5},{7,6},{8,7},{9,8},{10,9... | collective-permute-start | bytes 786440 | tf_op jit(solution)/shard_map/ppermute | solution.py:471
  27.5 3.6 %smooth_own.1 = (f32[4,2048,128]{2,1,0:T(8,128)S(1)}, f32[2,512,128]{2,1,0:T(8,128)S(1)}) custom-call(f32[4,2048,128]{2,1,0:T(8,128)S(1)} %get-tuple-element.30.r_v, f32[4,2112,128]{2,1,0:T(8,128)S(1)} %get-tuple-element.32.g_s, f32[4,2048,128]{2,1,0:T(8,128)S(1)} %get-tuple-element.33.i_s, f32[2,512,128]{2,1,0:T(8,128)S(1)} %get-tuple-element.34.rm, ...), custom_call_target="tpu_custom_call" | custom-call | flops 20000000 | tf_op jit(solution)/shard_map/smooth_own/pallas_call | solution.py:496
  31.2 0.0 collective-permute-done.4.rxa
  31.2 0.0 collective-permute-done.5.rxb
  31.2 1.4 %solve_coarse.1 = (f32[2,1024,128]{2,1,0:T(8,128)S(1)}, f32[2,192,128]{2,1,0:T(8,128)S(1)}, f32[8,128]{1,0:T(8,128)S(1)}) custom-call(f32[2,512,128]{2,1,0:T(8,128)S(1)} %get-tuple-element.38.s1, f32[128,128]{1,0:T(8,128)S(1)} %get-tuple-element.39.s2, f32[2,504,128]{2,1,0:T(8,128)S(1)} %get-tuple-element.40.fx, f32[528,128]{1,0:T(8,128)S(1)} %get-tuple-element.41.sya, ...), custom_call_target="tpu_custom_call" | custom-call | flops 20000000 | tf_op jit(solution)/shard_map/solve_coarse/pallas_call | solution.py:518
  32.6 1.2 %collective-permute-done.7.rzb = f32[512,128]{1,0:T(8,128)S(1)} collective-permute-done((f32[512,128]{1,0:T(8,128)S(1)}, f32[512,128]{1,0:T(8,128)S(1)}, u32[]{:S(2)}, u32[]{:S(2)}) %collective-permute-start.7) | collective-permute-done | bytes 262176 | tf_op jit(solution)/shard_map/ppermute | solution.py:471
  33.7 0.0 collective-permute-done.6.rza
  33.7 5.7 %solve_fine.1 = (f32[4,2112,128]{2,1,0:T(8,128)S(1)}, f32[2048,512]{1,0:T(8,128)S(1)}, f32[128,8]{1,0:T(8,128)S(1)}) custom-call(f32[4,2048,128]{2,1,0:T(8,128)S(1)} %get-tuple-element.30.r_v, f32[4,2048,128]{2,1,0:T(8,128)S(1)} %get-tuple-element.31.d_v, f32[4,2048,128]{2,1,0:T(8,128)S(1)} %get-tuple-element.37.s0, ...), custom_call_target="tpu_custom_call" | custom-call | tf_op jit(solution)/shard_map/solve_fine/pallas_call | solution.py:529
  39.4 18.7 %all_to_all.11 = f32[128,1,8]{2,1,0:T(1,128)S(1)} all-to-all(f32[128,1,8]{2,1,0:T(1,128)S(1)} %bitcast.9), channel_id=1, replica_groups=mesh['gx'=8,'gy'=16] {'gx','gy'}, dimensions={0} | all-to-all | bytes 8192 | tf_op jit(solution)/shard_map/all_to_all | solution.py:540
  58.2 4.3 %scale_outputs.1 = (f32[2048,512]{1,0:T(8,128)}, f32[2048,512]{1,0:T(8,128)}) custom-call(f32[128,8]{1,0:T(8,128)S(1)} %bitcast.8, f32[4,2048,128]{2,1,0:T(8,128)S(1)} %get-tuple-element.30.r_v, f32[4,2048,128]{2,1,0:T(8,128)S(1)} %get-tuple-element.31.d_v, f32[4,2112,128]{2,1,0:T(8,128)S(1)} %get-tuple-element.54.p, f32[2048,512]{1,0:T(8,128)S(1)} %get-tuple-element.55.im), custom_call_target="tpu_custom_call" | custom-call | tf_op jit(solution)/shard_map/scale_outputs/pallas_call | solution.py:542
Async XLA Ops:
  6.2 13.5 %collective-permute-start.1 = (f32[528,128]{1,0:T(8,128)S(1)}, f32[528,128]{1,0:T(8,128)S(1)}, u32[]{:S(2)}, u32[]{:S(2)}) collective-permute-start(f32[528,128]{1,0:T(8,128)S(1)} %get-tuple-element.41.sya), channel_id=1, source_target_pairs={{0,1},{1,2},{2,3},{3,4},{4,5},{5,6},{6,7},{7,8},{8,9},{9,10},{10,1... | collective-permute-start | bytes 811016 | tf_op jit(solution)/shard_map/ppermute | solution.py:471
  8.7 11.0 %collective-permute-start = (f32[528,128]{1,0:T(8,128)S(1)}, f32[528,128]{1,0:T(8,128)S(1)}, u32[]{:S(2)}, u32[]{:S(2)}) collective-permute-start(f32[528,128]{1,0:T(8,128)S(1)} %get-tuple-element.42.syb), channel_id=1, source_target_pairs={{0,15},{1,0},{2,1},{3,2},{4,3},{5,4},{6,5},{7,6},{8,7},{9,8},{10,9... | collective-permute-start | bytes 811016 | tf_op jit(solution)/shard_map/ppermute | solution.py:471
  13.1 6.5 %collective-permute-start.3 = (f32[32,128]{1,0:T(8,128)S(1)}, f32[32,128]{1,0:T(8,128)S(1)}, u32[]{:S(2)}, u32[]{:S(2)}) collective-permute-start(f32[32,128]{1,0:T(8,128)S(1)} %get-tuple-element.43.core), channel_id=1, source_target_pairs={{0,2},{1,3},{2,4},{3,5},{4,6},{5,7},{6,8},{7,9},{8,10},{9,11},{10,... | collective-permute-start | bytes 49160 | tf_op jit(solution)/shard_map/ppermute | solution.py:471
  13.1 6.5 %collective-permute-start.2 = (f32[32,128]{1,0:T(8,128)S(1)}, f32[32,128]{1,0:T(8,128)S(1)}, u32[]{:S(2)}, u32[]{:S(2)}) collective-permute-start(f32[32,128]{1,0:T(8,128)S(1)} %get-tuple-element.43.core), channel_id=1, source_target_pairs={{0,14},{1,15},{2,0},{3,1},{4,2},{5,3},{6,4},{7,5},{8,6},{9,7},{10,... | collective-permute-start | bytes 49160 | tf_op jit(solution)/shard_map/ppermute | solution.py:471
  19.7 11.4 %collective-permute-start.4 = (f32[680,128]{1,0:T(8,128)S(1)}, f32[680,128]{1,0:T(8,128)S(1)}, u32[]{:S(2)}, u32[]{:S(2)}) collective-permute-start(f32[680,128]{1,0:T(8,128)S(1)} %get-tuple-element.45), channel_id=1, source_target_pairs={{0,112},{16,0},{32,16},{48,32},{64,48},{80,64},{96,80},{112,96},{1... | collective-permute-start | bytes 1044488 | tf_op jit(solution)/shard_map/ppermute | solution.py:471
  21.5 9.7 %collective-permute-start.5 = (f32[680,128]{1,0:T(8,128)S(1)}, f32[680,128]{1,0:T(8,128)S(1)}, u32[]{:S(2)}, u32[]{:S(2)}) collective-permute-start(f32[680,128]{1,0:T(8,128)S(1)} %get-tuple-element.46), channel_id=1, source_target_pairs={{0,16},{16,32},{32,48},{48,64},{64,80},{80,96},{96,112},{112,0},{1... | collective-permute-start | bytes 1044488 | tf_op jit(solution)/shard_map/ppermute | solution.py:471
  22.7 11.0 %collective-permute-start.7 = (f32[512,128]{1,0:T(8,128)S(1)}, f32[512,128]{1,0:T(8,128)S(1)}, u32[]{:S(2)}, u32[]{:S(2)}) collective-permute-start(f32[512,128]{1,0:T(8,128)S(1)} %get-tuple-element.51.sza), channel_id=1, source_target_pairs={{0,1},{1,2},{2,3},{3,4},{4,5},{5,6},{6,7},{7,8},{8,9},{9,10},{10,1... | collective-permute-start | bytes 786440 | tf_op jit(solution)/shard_map/ppermute | solution.py:471
  22.7 11.0 %collective-permute-start.6 = (f32[512,128]{1,0:T(8,128)S(1)}, f32[512,128]{1,0:T(8,128)S(1)}, u32[]{:S(2)}, u32[]{:S(2)}) collective-permute-start(f32[512,128]{1,0:T(8,128)S(1)} %get-tuple-element.52.szb), channel_id=1, source_target_pairs={{0,15},{1,0},{2,1},{3,2},{4,3},{5,4},{6,5},{7,6},{8,7},{9,8},{10,9... | collective-permute-start | bytes 786440 | tf_op jit(solution)/shard_map/ppermute | solution.py:471

commit v2 on v1

--- a/solution.py
+++ b/solution.py
@@ -192,7 +192,7 @@
         send(sya, syb, pl.ds(YL + a * 16, 16), ref[pl.ds(shift, 16, 8), :], ref[pl.ds(7 - shift, 16, 8), :])
 
 
-def smooth_kernel(r_v, g_s, i_s, rm, gm, im, s0, s1):
+def smooth_kernel(r_v, g_s, i_s, rm, gm, im, sza, szb, rya, ryb, s0, s1):
     def middle(i, carry):
         rows = pl.ds(16 * i, 16)
         c = take(gm, pl.ds(16 * i + 16, 16))
@@ -210,6 +210,11 @@
         return carry
 
     lax.fori_loop(0, X, fine, 0, unroll=8)
+    halo = Halo(sz=(sza, szb), ry=(rya, ryb))
+    for hi in range(2):
+        for k in range(4):
+            rows = pl.ds(hi * (Y - 1), X, Y)
+            s0[k, rows, :] = s0[k, rows, :] + halo.get("sz", hi, k * X, X) * halo.get("ry", hi, YF + k * X, X)
 
 
 class Halo:
@@ -370,9 +375,9 @@
             fm[k, pl.ds(base + 1, n1, 2), :] = mid
 
 
-def fine_kernel(r_v, d_v, s0, rep_m, fm, left_in, part, fx, sya, syb, sza, szb, rya, ryb, rza, rzb, rxa, rxb,
+def fine_kernel(r_v, d_v, s0, rep_m, fm, left_in, part, fx, sya, syb, rya, ryb, rza, rzb, rxa, rxb,
                 p, im, sums, hy):
-    halo = Halo(sy=(sya, syb), sz=(sza, szb), rx=(rxa, rxb), ry=(rya, ryb), rz=(rza, rzb))
+    halo = Halo(sy=(sya, syb), rx=(rxa, rxb), ry=(rya, ryb), rz=(rza, rzb))
     twice = doubling(256, Z)
 
     def spread(i, carry):
@@ -387,11 +392,6 @@
         for k in range(4):
             rows = pl.ds(Y + hi * (X - 1) * Y, Y)
             p[k, rows, :] = p[k, rows, :] + fx[hi, pl.ds(XF + (4 + k) * Y, Y), :] * halo.get("rx", hi, XF + k * Y, Y)
-    for hi in range(2):
-        for k in range(4):
-            rows = pl.ds(Y + hi * (Y - 1), X, Y)
-            p[k, rows, :] = p[k, rows, :] + halo.get("sz", hi, k * X, X) * halo.get("ry", hi, YF + k * X, X)
-
     outer = times(take(fm, pl.ds(0, 2 * (X + Y))), twice)
     for (along_y, hi), base in zip(FACES, FACE_ROWS):
         n = X if along_y else Y
@@ -495,13 +495,13 @@
     r2b = shift(core, "gy", 2)
     s0, s1 = pl.pallas_call(
         smooth_kernel,
-        in_specs=[VM] * 6,
+        in_specs=[VM] * 10,
         out_specs=[VM] * 2,
         out_shape=[resident(4, X * Y, LANES), resident(2, 512, LANES)],
         compiler_params=pltpu.CompilerParams(vmem_limit_bytes=4 * 2**20),
         cost_estimate=pl.CostEstimate(flops=COST, transcendentals=0, bytes_accessed=0),
         name="smooth_own",
-    )(in_vmem(r_v), in_vmem(g), in_vmem(inv), in_vmem(rm), in_vmem(gm), in_vmem(im1))
+    )(in_vmem(r_v), in_vmem(g), in_vmem(inv), in_vmem(rm), in_vmem(gm), in_vmem(im1), in_vmem(sza), in_vmem(szb), rya, ryb)
     block, outa, outb = pl.pallas_call(
         pack_kernel,
         in_specs=[VM] * 6,
@@ -528,14 +528,14 @@
     )(in_vmem(s1), in_vmem(s2), in_vmem(fx), in_vmem(sya), in_vmem(syb), in_vmem(block), rya, ryb, rxa, rxb)
     p, im, sums = pl.pallas_call(
         fine_kernel,
-        in_specs=[VM] * 18,
+        in_specs=[VM] * 16,
         out_specs=[VM] * 3,
         out_shape=[resident(4, (X + 2) * Y, LANES), resident(X * Y, Z), f32(LANES, 8)],
         scratch_shapes=[vm((2, X, Z), F32)],
         compiler_params=pltpu.CompilerParams(vmem_limit_bytes=8 * 2**20),
         name="solve_fine",
     )(in_vmem(r_v), in_vmem(d_v), in_vmem(s0), in_vmem(rep), in_vmem(faces), in_vmem(left),
-      in_vmem(part), in_vmem(fx), in_vmem(sya), in_vmem(syb), in_vmem(sza), in_vmem(szb), rya, ryb, rza, rzb, rxa, rxb)
+      in_vmem(part), in_vmem(fx), in_vmem(sya), in_vmem(syb), rya, ryb, rza, rzb, rxa, rxb)
 
     every = lax.all_to_all(sums, ("gx", "gy"), 0, 0, tiled=True)
     blocks = pl.BlockSpec((OUT * Y, Z), lambda i: (i, 0))

time: 62.6 us -> 62.4 us (level)
  waiting for transfers between devices: 2.67 us -> 12.5 us
  starting transfers between devices: 19.8 us -> 14.6 us
  blocking collectives: 18.7 us -> 14.2 us
    ppermute x8, waiting for transfers between devices: 2.67 us -> 12.5 us  [shift(): lax.ppermute(value, axis, [(i, (i + distance) % count) for i in range(cou...]
    ppermute x8, starting transfers between devices: 19.8 us -> 14.6 us  [shift(): lax.ppermute(value, axis, [(i, (i + distance) % count) for i in range(cou...]
    all_to_all x1, blocking collectives: 18.7 us -> 14.2 us  [body(): every = lax.all_to_all(sums, ('gx', 'gy'), 0, 0, tiled=True)]
  transfers between devices with their start and end apart: 8 -> 8, of which waited for: 2 -> 5; matrix products, arithmetic and copies ran while one was open for 0% -> 0% of each run, Pallas kernels for 8% -> 9%
where the time goes in v2:
time: 62.4 us; the launch traced here: 62.3 us
  Pallas kernels  20.4 us (33%)
  starting transfers between devices  14.6 us (23%)
  blocking collectives  14.2 us (23%)
  waiting for transfers between devices  12.5 us (20%)
  between operations  0.69 us (1%)
    ppermute x8, starting transfers between devices, shift(): lax.ppermute(value, axis, [(i, (i + distance) % count) for i in range(cou...  14.6 us
    all_to_all x1, blocking collectives, body(): every = lax.all_to_all(sums, ('gx', 'gy'), 0, 0, tiled=True)  14.2 us
    ppermute x8, waiting for transfers between devices, shift(): lax.ppermute(value, axis, [(i, (i + distance) % count) for i in range(cou...  12.5 us
    pallas_call x1, Pallas kernels, body(): pl.pallas_call(restrict_kernel, in_specs=[hbm, hbm], out_specs=[VM] * 15,...  5.55 us
    pallas_call x1, Pallas kernels, body(): pl.pallas_call(fine_kernel, in_specs=[VM] * 16, out_specs=[VM] * 3, out_s...  5.12 us
    pallas_call x1, Pallas kernels, body(): pl.pallas_call(final_kernel, grid=(X // OUT,), in_specs=[VM] * 5, out_spe...  4.27 us
    pallas_call x1, Pallas kernels, body(): pl.pallas_call(smooth_kernel, in_specs=[VM] * 10, out_specs=[VM] * 2, out...  4 us
    pallas_call x1, Pallas kernels, body(): pl.pallas_call(coarse_kernel, in_specs=[VM] * 10, out_specs=[VM] * 3, out...  1.37 us
  transfers between devices with their start and end apart: 8, of which 5 were waited for; matrix products, arithmetic and copies ran while one was open for 0% of the time, Pallas kernels for 9%

profile of v2, /device:TPU:1, one launch (start us, length us, event | category | flops | bytes accessed | tf_op | source)
XLA Modules:
  0.0 62.3 jit_solution(4458497039771415811)
XLA Ops:
  0.6 5.5 %restrict_all.1 = (f32[4,2048,128]{2,1,0:T(8,128)S(1)}, f32[4,2048,128]{2,1,0:T(8,128)S(1)}, f32[4,2112,128]{2,1,0:T(8,128)S(1)}, f32[4,2048,128]{2,1,0:T(8,128)...) custom-call(f32[2048,512]{1,0:T(8,128)} %bitcast.10, ...), custom_call_target="tpu_custom_call" | custom-call | tf_op jit(solution)/shard_map/restrict_all/pallas_call | solution.py:479
  6.2 6.8 %collective-permute-start = (f32[528,128]{1,0:T(8,128)S(1)}, f32[528,128]{1,0:T(8,128)S(1)}, u32[]{:S(2)}, u32[]{:S(2)}) collective-permute-start(f32[528,128]{1,0:T(8,128)S(1)} %get-tuple-element.39.syb), channel_id=1, source_target_pairs={{0,15},{1,0},{2,1},{3,2},{4,3},{5,4},{6,5},{7,6},{8,7},{9,8},{10,9... | collective-permute-start | bytes 811016 | tf_op jit(solution)/shard_map/ppermute | solution.py:471
  13.0 0.0 collective-permute-start.1
  13.0 1.3 %collective-permute-start.2 = (f32[32,128]{1,0:T(8,128)S(1)}, f32[32,128]{1,0:T(8,128)S(1)}, u32[]{:S(2)}, u32[]{:S(2)}) collective-permute-start(f32[32,128]{1,0:T(8,128)S(1)} %get-tuple-element.45.core), channel_id=1, source_target_pairs={{0,14},{1,15},{2,0},{3,1},{4,2},{5,3},{6,4},{7,5},{8,6},{9,7},{10,... | collective-permute-start | bytes 49160 | tf_op jit(solution)/shard_map/ppermute | solution.py:471
  14.3 1.7 %collective-permute-start.3 = (f32[32,128]{1,0:T(8,128)S(1)}, f32[32,128]{1,0:T(8,128)S(1)}, u32[]{:S(2)}, u32[]{:S(2)}) collective-permute-start(f32[32,128]{1,0:T(8,128)S(1)} %get-tuple-element.45.core), channel_id=1, source_target_pairs={{0,2},{1,3},{2,4},{3,5},{4,6},{5,7},{6,8},{7,9},{8,10},{9,11},{10,... | collective-permute-start | bytes 49160 | tf_op jit(solution)/shard_map/ppermute | solution.py:471
  16.0 2.5 %collective-permute-done.2.r2a = f32[32,128]{1,0:T(8,128)S(1)} collective-permute-done((f32[32,128]{1,0:T(8,128)S(1)}, f32[32,128]{1,0:T(8,128)S(1)}, u32[]{:S(2)}, u32[]{:S(2)}) %collective-permute-start.2) | collective-permute-done | bytes 16416 | tf_op jit(solution)/shard_map/ppermute | solution.py:471
  18.5 2.3 %collective-permute-done.3.r2b = f32[32,128]{1,0:T(8,128)S(1)} collective-permute-done((f32[32,128]{1,0:T(8,128)S(1)}, f32[32,128]{1,0:T(8,128)S(1)}, u32[]{:S(2)}, u32[]{:S(2)}) %collective-permute-start.3) | collective-permute-done | bytes 16416 | tf_op jit(solution)/shard_map/ppermute | solution.py:471
  20.9 0.0 collective-permute-done.rya
  20.9 2.8 %collective-permute-done.1.ryb = f32[528,128]{1,0:T(8,128)S(1)} collective-permute-done((f32[528,128]{1,0:T(8,128)S(1)}, f32[528,128]{1,0:T(8,128)S(1)}, u32[]{:S(2)}, u32[]{:S(2)}) %collective-permute-start.1) | collective-permute-done | bytes 270368 | tf_op jit(solution)/shard_map/ppermute | solution.py:471
  23.7 0.1 pack_faces.1
  23.8 2.1 %collective-permute-start.4 = (f32[680,128]{1,0:T(8,128)S(1)}, f32[680,128]{1,0:T(8,128)S(1)}, u32[]{:S(2)}, u32[]{:S(2)}) collective-permute-start(f32[680,128]{1,0:T(8,128)S(1)} %get-tuple-element.47), channel_id=1, source_target_pairs={{0,112},{16,0},{32,16},{48,32},{64,48},{80,64},{96,80},{112,96},{1... | collective-permute-start | bytes 1044488 | tf_op jit(solution)/shard_map/ppermute | solution.py:471
  25.9 1.2 %collective-permute-start.5 = (f32[680,128]{1,0:T(8,128)S(1)}, f32[680,128]{1,0:T(8,128)S(1)}, u32[]{:S(2)}, u32[]{:S(2)}) collective-permute-start(f32[680,128]{1,0:T(8,128)S(1)} %get-tuple-element.48), channel_id=1, source_target_pairs={{0,16},{16,32},{32,48},{48,64},{64,80},{80,96},{96,112},{112,0},{1... | collective-permute-start | bytes 1044488 | tf_op jit(solution)/shard_map/ppermute | solution.py:471
  27.1 0.6 %collective-permute-start.6 = (f32[512,128]{1,0:T(8,128)S(1)}, f32[512,128]{1,0:T(8,128)S(1)}, u32[]{:S(2)}, u32[]{:S(2)}) collective-permute-start(f32[512,128]{1,0:T(8,128)S(1)} %get-tuple-element.38.szb), channel_id=1, source_target_pairs={{0,15},{1,0},{2,1},{3,2},{4,3},{5,4},{6,5},{7,6},{8,7},{9,8},{10,9... | collective-permute-start | bytes 786440 | tf_op jit(solution)/shard_map/ppermute | solution.py:471
  27.7 0.9 %collective-permute-start.7 = (f32[512,128]{1,0:T(8,128)S(1)}, f32[512,128]{1,0:T(8,128)S(1)}, u32[]{:S(2)}, u32[]{:S(2)}) collective-permute-start(f32[512,128]{1,0:T(8,128)S(1)} %get-tuple-element.37.sza), channel_id=1, source_target_pairs={{0,1},{1,2},{2,3},{3,4},{4,5},{5,6},{6,7},{7,8},{8,9},{9,10},{10,1... | collective-permute-start | bytes 786440 | tf_op jit(solution)/shard_map/ppermute | solution.py:471
  28.6 4.0 %smooth_own.1 = (f32[4,2048,128]{2,1,0:T(8,128)S(1)}, f32[2,512,128]{2,1,0:T(8,128)S(1)}) custom-call(f32[4,2048,128]{2,1,0:T(8,128)S(1)} %get-tuple-element.30.r_v, f32[4,2112,128]{2,1,0:T(8,128)S(1)} %get-tuple-element.32.g_s, f32[4,2048,128]{2,1,0:T(8,128)S(1)} %get-tuple-element.33.i_s, f32[2,512,128]{2,1,0:T(8,128)S(1)} %get-tuple-element.34.rm, ...), custom_call_target="tpu_custom_call" | custom-call | flops 20000000 | tf_op jit(solution)/shard_map/smooth_own/pallas_call | solution.py:496
  32.6 0.0 collective-permute-done.4.rxa
  32.6 0.0 collective-permute-done.5.rxb
  32.6 1.4 %solve_coarse.1 = (f32[2,1024,128]{2,1,0:T(8,128)S(1)}, f32[2,192,128]{2,1,0:T(8,128)S(1)}, f32[8,128]{1,0:T(8,128)S(1)}) custom-call(f32[2,512,128]{2,1,0:T(8,128)S(1)} %get-tuple-element.42.s1, f32[128,128]{1,0:T(8,128)S(1)} %get-tuple-element.43.s2, f32[2,504,128]{2,1,0:T(8,128)S(1)} %get-tuple-element.44.fx, f32[528,128]{1,0:T(8,128)S(1)} %get-tuple-element.40.sya, ...), custom_call_target="tpu_custom_call" | custom-call | flops 20000000 | tf_op jit(solution)/shard_map/solve_coarse/pallas_call | solution.py:518
  34.0 1.2 %collective-permute-done.6.rza = f32[512,128]{1,0:T(8,128)S(1)} collective-permute-done((f32[512,128]{1,0:T(8,128)S(1)}, f32[512,128]{1,0:T(8,128)S(1)}, u32[]{:S(2)}, u32[]{:S(2)}) %collective-permute-start.6) | collective-permute-done | bytes 262176 | tf_op jit(solution)/shard_map/ppermute | solution.py:471
  35.1 3.6 %collective-permute-done.7.rzb = f32[512,128]{1,0:T(8,128)S(1)} collective-permute-done((f32[512,128]{1,0:T(8,128)S(1)}, f32[512,128]{1,0:T(8,128)S(1)}, u32[]{:S(2)}, u32[]{:S(2)}) %collective-permute-start.7) | collective-permute-done | bytes 262176 | tf_op jit(solution)/shard_map/ppermute | solution.py:471
  38.7 5.1 %solve_fine.1 = (f32[4,2112,128]{2,1,0:T(8,128)S(1)}, f32[2048,512]{1,0:T(8,128)S(1)}, f32[128,8]{1,0:T(8,128)S(1)}) custom-call(f32[4,2048,128]{2,1,0:T(8,128)S(1)} %get-tuple-element.30.r_v, f32[4,2048,128]{2,1,0:T(8,128)S(1)} %get-tuple-element.31.d_v, f32[4,2048,128]{2,1,0:T(8,128)S(1)} %get-tuple-element.41.s0, ...), custom_call_target="tpu_custom_call" | custom-call | tf_op jit(solution)/shard_map/solve_fine/pallas_call | solution.py:529
  43.8 14.2 %all_to_all.11 = f32[128,1,8]{2,1,0:T(1,128)S(1)} all-to-all(f32[128,1,8]{2,1,0:T(1,128)S(1)} %bitcast.9), channel_id=1, replica_groups=mesh['gx'=8,'gy'=16] {'gx','gy'}, dimensions={0} | all-to-all | bytes 8192 | tf_op jit(solution)/shard_map/all_to_all | solution.py:540
  58.0 4.3 %scale_outputs.1 = (f32[2048,512]{1,0:T(8,128)}, f32[2048,512]{1,0:T(8,128)}) custom-call(f32[128,8]{1,0:T(8,128)S(1)} %bitcast.8, f32[4,2048,128]{2,1,0:T(8,128)S(1)} %get-tuple-element.30.r_v, f32[4,2048,128]{2,1,0:T(8,128)S(1)} %get-tuple-element.31.d_v, f32[4,2112,128]{2,1,0:T(8,128)S(1)} %get-tuple-element.54.p, f32[2048,512]{1,0:T(8,128)S(1)} %get-tuple-element.55.im), custom_call_target="tpu_custom_call" | custom-call | tf_op jit(solution)/shard_map/scale_outputs/pallas_call | solution.py:542
Async XLA Ops:
  6.2 14.7 %collective-permute-start = (f32[528,128]{1,0:T(8,128)S(1)}, f32[528,128]{1,0:T(8,128)S(1)}, u32[]{:S(2)}, u32[]{:S(2)}) collective-permute-start(f32[528,128]{1,0:T(8,128)S(1)} %get-tuple-element.39.syb), channel_id=1, source_target_pairs={{0,15},{1,0},{2,1},{3,2},{4,3},{5,4},{6,5},{7,6},{8,7},{9,8},{10,9... | collective-permute-start | bytes 811016 | tf_op jit(solution)/shard_map/ppermute | solution.py:471
  13.0 10.7 %collective-permute-start.1 = (f32[528,128]{1,0:T(8,128)S(1)}, f32[528,128]{1,0:T(8,128)S(1)}, u32[]{:S(2)}, u32[]{:S(2)}) collective-permute-start(f32[528,128]{1,0:T(8,128)S(1)} %get-tuple-element.40.sya), channel_id=1, source_target_pairs={{0,1},{1,2},{2,3},{3,4},{4,5},{5,6},{6,7},{7,8},{8,9},{9,10},{10,1... | collective-permute-start | bytes 811016 | tf_op jit(solution)/shard_map/ppermute | solution.py:471
  13.0 5.5 %collective-permute-start.2 = (f32[32,128]{1,0:T(8,128)S(1)}, f32[32,128]{1,0:T(8,128)S(1)}, u32[]{:S(2)}, u32[]{:S(2)}) collective-permute-start(f32[32,128]{1,0:T(8,128)S(1)} %get-tuple-element.45.core), channel_id=1, source_target_pairs={{0,14},{1,15},{2,0},{3,1},{4,2},{5,3},{6,4},{7,5},{8,6},{9,7},{10,... | collective-permute-start | bytes 49160 | tf_op jit(solution)/shard_map/ppermute | solution.py:471
  14.3 6.5 %collective-permute-start.3 = (f32[32,128]{1,0:T(8,128)S(1)}, f32[32,128]{1,0:T(8,128)S(1)}, u32[]{:S(2)}, u32[]{:S(2)}) collective-permute-start(f32[32,128]{1,0:T(8,128)S(1)} %get-tuple-element.45.core), channel_id=1, source_target_pairs={{0,2},{1,3},{2,4},{3,5},{4,6},{5,7},{6,8},{7,9},{8,10},{9,11},{10,... | collective-permute-start | bytes 49160 | tf_op jit(solution)/shard_map/ppermute | solution.py:471
  23.8 8.8 %collective-permute-start.4 = (f32[680,128]{1,0:T(8,128)S(1)}, f32[680,128]{1,0:T(8,128)S(1)}, u32[]{:S(2)}, u32[]{:S(2)}) collective-permute-start(f32[680,128]{1,0:T(8,128)S(1)} %get-tuple-element.47), channel_id=1, source_target_pairs={{0,112},{16,0},{32,16},{48,32},{64,48},{80,64},{96,80},{112,96},{1... | collective-permute-start | bytes 1044488 | tf_op jit(solution)/shard_map/ppermute | solution.py:471
  25.9 6.7 %collective-permute-start.5 = (f32[680,128]{1,0:T(8,128)S(1)}, f32[680,128]{1,0:T(8,128)S(1)}, u32[]{:S(2)}, u32[]{:S(2)}) collective-permute-start(f32[680,128]{1,0:T(8,128)S(1)} %get-tuple-element.48), channel_id=1, source_target_pairs={{0,16},{16,32},{32,48},{48,64},{64,80},{80,96},{96,112},{112,0},{1... | collective-permute-start | bytes 1044488 | tf_op jit(solution)/shard_map/ppermute | solution.py:471
  27.1 8.1 %collective-permute-start.6 = (f32[512,128]{1,0:T(8,128)S(1)}, f32[512,128]{1,0:T(8,128)S(1)}, u32[]{:S(2)}, u32[]{:S(2)}) collective-permute-start(f32[512,128]{1,0:T(8,128)S(1)} %get-tuple-element.38.szb), channel_id=1, source_target_pairs={{0,15},{1,0},{2,1},{3,2},{4,3},{5,4},{6,5},{7,6},{8,7},{9,8},{10,9... | collective-permute-start | bytes 786440 | tf_op jit(solution)/shard_map/ppermute | solution.py:471
  27.7 11.0 %collective-permute-start.7 = (f32[512,128]{1,0:T(8,128)S(1)}, f32[512,128]{1,0:T(8,128)S(1)}, u32[]{:S(2)}, u32[]{:S(2)}) collective-permute-start(f32[512,128]{1,0:T(8,128)S(1)} %get-tuple-element.37.sza), channel_id=1, source_target_pairs={{0,1},{1,2},{2,3},{3,4},{4,5},{5,6},{6,7},{7,8},{8,9},{9,10},{10,1... | collective-permute-start | bytes 786440 | tf_op jit(solution)/shard_map/ppermute | solution.py:471
